TPU v7x, 32 devices: a whole 2x2x4 slice. The times are simulated.
32 devices in a mesh: rows: 8 (over y, x, core), grp: 4 (over z).
Axes of the slice: x: 2, y: 2, z: 4, core: 2. Of those that a mesh axis runs over, the one named last changes fastest.
Arguments:
- matrix: bfloat16 [24576, 16384], P(('rows', 'grp')), may hold values from -3000 to 3000, as said below
- keep_mask: int32 [16, 24576], P(None, ('rows', 'grp')), may hold values 0 or 1
Outputs:
- cosine: float32 [16384, 256], P(('rows', 'grp'))
Inputs may be any that keep to these rules, and one draw needn't show every extreme that they name: `matrix`: entries are real-valued; row and column magnitudes vary.
All inputs are finite; a program needn't handle non-finite values. No bound on the sum of `keep_mask` on one device may be relied on, other than what follows from the above.
Results may differ from a plain program's by a relative error of at most 0.0003.
Values sent between devices are 32-bit elements; how exact they have to be, the bound alone decides.
A program may use at most 192 MiB of HBM per device.

v0:
```python
import jax
import jax.numpy as jnp
from jax import lax
from jax.sharding import PartitionSpec as P

WINDOW = 256


def shards(matrix, keep_mask):
    rows_here, columns = matrix.shape
    blocks = keep_mask.shape[0]
    width = columns // blocks
    count_outer = lax.axis_size("rows")
    count_inner = lax.axis_size("grp")
    tile = columns // (count_outer * count_inner)
    square = jnp.sum(jnp.square(matrix.astype(jnp.float32)), axis=0)
    gate = keep_mask.T.astype(jnp.bfloat16)
    masked = (matrix.reshape(rows_here, blocks, width) * gate[:, :, None]).reshape(
        rows_here, columns
    )
    panel = masked[:, :WINDOW]
    extra = (WINDOW + tile - 1) // tile
    padded = jnp.pad(square[:WINDOW], (0, extra * tile - WINDOW))
    spread = jnp.tile(padded.reshape(extra, tile).T, (columns // tile, 1))
    stats = jnp.concatenate([square[:, None], spread], axis=1)
    product = lax.dot_general(
        masked, panel, (((0,), (0,)), ((), ())), preferred_element_type=jnp.float32
    )
    partial_value = lax.psum_scatter(
        jnp.concatenate([product, stats], axis=1), "rows", scatter_dimension=0, tiled=True
    )
    result = lax.psum_scatter(partial_value, "grp", scatter_dimension=0, tiled=True)
    raw = result[:, :WINDOW]
    owned = result[:, WINDOW]
    window_sq = result[:, WINDOW + 1 :].T.reshape(-1)[:WINDOW]
    inverse_own = 1.0 / jnp.sqrt(owned + 1e-06)
    inverse_window = 1.0 / jnp.sqrt(window_sq + 1e-06)
    return raw * inverse_own[:, None] * inverse_window[None, :]


def solution(mesh):
    in_specs = (P(("rows", "grp"), None), P(None, ("rows", "grp")))
    out_specs = P(("rows", "grp"), None)
    return jax.shard_map(shards, mesh=mesh, in_specs=in_specs, out_specs=out_specs, check_vma=False)
```

profile of v0, /device:TPU:0, one launch (start us, length us, event | category | flops | bytes accessed | tf_op | source)
XLA Modules:
  0.0 270.5 jit_solution(7139497181866857384)
XLA Ops:
  6.5 0.0 copy-start
  6.5 0.0 reduce-scatter.3.cloned.1.call-start
  6.5 0.8 convert_bitcast_fusion
  7.4 10.2 %multiply_reduce_fusion = f32[16384]{0:T(1024)S(1)} fusion(bf16[768,16384]{1,0:T(8,128)(2,1)} %param.2), kind=kLoop, calls=%fused_computation | loop fusion | flops 37732352 | bytes 25231360 | tf_op jit(solution)/shard_map/reduce_sum | solution.py:16
  17.6 0.0 copy-done
  17.6 0.1 copy.6
  17.7 0.2 copy.3
  17.8 2.6 mul.29
  20.4 17.4 %copy.5 = bf16[96,8,16,1024]{3,1,2,0:T(8,128)(2,1)} copy(bf16[96,8,16,1024]{3,2,1,0:T(8,128)(2,1)S(1)} %bitcast.13) | data formatting | bytes 50331648
  37.8 26.9 %mul.31 = bf16[768,16384]{1,0:T(8,128)(2,1)} multiply(bf16[768,16384]{1,0:T(8,128)(2,1)} %param.2, bf16[768,16384]{1,0:T(8,128)(2,1)} %bitcast.14) | non-fusion elementwise | flops 12582912 | bytes 75497472 | tf_op jit(solution)/shard_map/mul | solution.py:18
  64.8 15.0 %fusion.1 = f32[16384,256]{0,1:T(8,128)} fusion(bf16[768,16384]{1,0:T(8,128)(2,1)} %mul.31), kind=kOutput, calls=%fused_computation.4 | convolution fusion | flops 6442450944 | bytes 42336256 | tf_op jit(solution)/shard_map/dot_general | solution.py:26
  79.8 11.7 %pad_maximum_fusion = f32[16384,258]{0,1:T(8,128)} fusion(f32[16384,1]{0,1:T(1,128)S(1)} %bitcast.16, f32[16384,1]{0,1:T(1,128)S(1)} %bitcast.15, f32[16384,256]{0,1:T(8,128)} %fusion.1), kind=kLoop, calls=%fused_computation.1 | loop fusion | flops 8454144 | bytes 33816576 | tf_op jit(solution)/shard_map/concatenate | solution.py:30
  91.5 0.0 reduce-scatter.3.cloned.1.call-update
  91.5 0.0 reduce-scatter.5.cloned.1.call-start
  91.6 121.5 %reduce-scatter.3.cloned.1.call-done = f32[2048,258]{0,1:T(8,128)} async-done(((f32[16384,258]{0,1:T(8,128)}), f32[2048,258]{0,1:T(8,128)}) %reduce-scatter.3.cloned.1.call-update) | async-done | bytes 2113552 | tf_op jit(solution)/shard_map/reduce_scatter | solution.py:29
  213.1 0.0 reduce-scatter.5.cloned.1.call-update
  213.1 47.0 %reduce-scatter.5.cloned.1.call-done = f32[512,258]{0,1:T(8,128)} async-done(((f32[2048,258]{0,1:T(8,128)}), f32[512,258]{0,1:T(8,128)}) %reduce-scatter.5.cloned.1.call-update) | async-done | bytes 528400 | tf_op jit(solution)/shard_map/reduce_scatter | solution.py:32
  260.1 0.7 fusion.4
  260.8 0.7 fusion.3
  261.5 1.1 fusion
  262.6 1.0 copy.4
  (2 shorter events, 0.0 us)
Async XLA Ops:
  6.5 11.0 %copy-start = (pred[512]{0:T(512)(128)(4,1)S(1)}, pred[512]{0:T(512)(128)(4,1)}, u32[]{:S(2)}) copy-start(pred[512]{0:T(512)(128)(4,1)} %constant.4.clone.1) | copy-start | bytes 1540
  6.5 206.5 %reduce-scatter.3.cloned.1.call-start = ((), (), s32[]{:S(2)}) async-start(), calls=%async_computation.2 | async-start | bytes 19464192 | tf_op jit(solution)/shard_map/reduce_scatter | solution.py:29
  91.5 168.5 %reduce-scatter.5.cloned.1.call-start = ((), (), s32[]{:S(2)}) async-start(), calls=%async_computation.3 | async-start | bytes 2703360 | tf_op jit(solution)/shard_map/reduce_scatter | solution.py:32
Sparse Core Ops, SparseCore 0:
  91.7 121.3 reduce-scatter.2
  215.4 44.6 reduce-scatter.4
where the time goes:
time: 271 us; the launch traced here: 270 us
  waiting for transfers between devices  168 us (62%)
  other arithmetic  52.2 us (19%)
  local copies, waits for them, and re-layouts  21.2 us (8%)
  matrix products  15 us (6%)
  between operations  13.5 us (5%)
    reduce_scatter x1, waiting for transfers between devices, shards(): lax.psum_scatter(jnp.concatenate([product, stats], axis=1), 'rows', scatt...  121 us
    reduce_scatter x1, waiting for transfers between devices, shards(): lax.psum_scatter(partial_value, 'grp', scatter_dimension=0, tiled=True)  47 us
    mul x1, other arithmetic, shards(): matrix.reshape(rows_here, blocks, width) * gate[:, :, None]  26.9 us
    unnamed x5, local copies, waits for them, and re-layouts  17.5 us
    dot_general x1, matrix products, shards(): lax.dot_general(masked, panel, (((0,), (0,)), ((), ())), preferred_elemen...  15 us
    concatenate x1, other arithmetic, shards(): jnp.concatenate([product, stats], axis=1)  11.7 us
    reduce_sum x1, other arithmetic, shards(): square = jnp.sum(jnp.square(matrix.astype(jnp.float32)), axis=0)  10.2 us
  transfers between devices with their start and end apart: 2, of which 2 were waited for; matrix products, arithmetic and copies ran while one was open for 0% of the time, Pallas kernels for 0%

commit v1 on v0

v1 whole, which is shorter than its diff:
```python
import functools

import jax
import jax.numpy as jnp
from jax import lax
from jax.experimental import pallas as pl
from jax.experimental.pallas import tpu as pltpu
from jax.sharding import PartitionSpec as P

WINDOW = 256
STAT = 8
HEIGHT = WINDOW + STAT
SUB = 256
SLOTS = 3
MESH = pl.DeviceIdType.MESH
PIECES_XYZ = (32, 32, 24, 16, 16)
PIECES_YXZ = (32, 24, 24, 16, 16)
PIECES_Z = (("zxy", 16), ("zyx", 16))
EARLY = 2


class Piece:
    def __init__(self, start, height, order):
        self.start, self.height, self.order = start, height, order


def pieces():
    out, at = [], 0
    for order, height in (
        [("xyz", h) for h in PIECES_XYZ]
        + [("yxz", h) for h in PIECES_YXZ]
        + list(PIECES_Z)
    ):
        out.append((at, height, order))
        at += height
    assert at == HEIGHT
    made = [Piece(*p) for p in out]
    a = len(PIECES_XYZ)
    b = a + len(PIECES_YXZ)
    return made[:a], made[a:b], made[b:]


def phase_copies(order, phase, sizes):
    axis, fixed = order[phase], order[:phase]
    groups = [
        (dx, dy)
        for dx in reversed(range(sizes["x"]))
        for dy in reversed(range(sizes["y"]))
        if not ("x" in fixed and dx) and not ("y" in fixed and dy)
    ]
    kept = [g for g in groups if axis == "z" or g["xy".index(axis)] == 0]
    sent = []
    for d in range(1, sizes[axis]):
        if axis == "z":
            sent.append(kept)
        elif axis == "x":
            sent.append([(d, dy) for _, dy in kept])
        else:
            sent.append([(dx, d) for dx, _ in kept])
    return axis, kept, sent


def kernel(cfg, matrix_ref, keep_ref, out_ref, acc, sib_out, sib_in, mbuf, panel,
           masked, wst, load_sem, sib_send, sib_recv, send_sem, recv_sem, *bufs):
    X, Y, Z, tile, width, step = (
        cfg["x"], cfg["y"], cfg["z"], cfg["tile"], cfg["width"], cfg["step"]
    )
    span = Z * tile
    halves = span // step
    rows = lax.axis_index("rows")
    z = lax.axis_index("grp")
    c = lax.rem(rows, 2)
    x = lax.rem(rows // 2, X)
    y = rows // (2 * X)

    def device(yy, xx, cc, zz):
        return ((yy * X + xx) * 2 + cc, zz)

    def quad(g):
        return lax.rem(y + g[1], Y) * X + lax.rem(x + g[0], X)

    def peer(axis, d):
        if axis == "x":
            return device(y, lax.rem(x + d, X), c, z)
        if axis == "y":
            return device(lax.rem(y + d, Y), x, c, z)
        return device(y, x, c, lax.rem(z + d, Z))

    groups = [(dx, dy) for dx in reversed(range(X)) for dy in reversed(range(Y))]
    steps = []
    for gi, g in enumerate(groups):
        for own in (0, 1):
            for h in range(halves):
                steps.append((gi, g, own, h))

    def base(s):
        _, g, own, h = s
        cc = c if own else 1 - c
        return pl.multiple_of((quad(g) * 2 + cc) * span + h * step, step)

    def load(i):
        return pltpu.make_async_copy(
            matrix_ref.at[:, pl.ds(base(steps[i]), step)],
            mbuf.at[i % SLOTS],
            load_sem.at[i % SLOTS],
        )

    window = pltpu.make_async_copy(
        matrix_ref.at[:, pl.ds(0, WINDOW)],
        mbuf.at[SLOTS - 1, :, pl.ds(0, WINDOW)],
        load_sem.at[SLOTS - 1],
    )
    window.start()
    for i in range(SLOTS - 1):
        load(i).start()

    peers = [device(y, x, 1 - c, z)]
    for axis, n in (("x", X), ("y", Y), ("z", Z)):
        peers += [peer(axis, d) for d in range(1, n)]
    barrier = pltpu.get_barrier_semaphore()
    for p in peers:
        pl.semaphore_signal(barrier, inc=1, device_id=p, device_id_type=MESH)

    window.wait()
    first = mbuf[SLOTS - 1, :, pl.ds(0, WINDOW)].astype(jnp.float32)
    window_sq = jnp.sum(first * first, axis=0, keepdims=True)
    panel[...] = first.T * keep_ref[pl.ds(0, 1), :].astype(jnp.float32)
    extra = (WINDOW + tile - 1) // tile
    wst[...] = jnp.zeros_like(wst)
    for e in range(extra):
        part = window_sq[:, e * tile : min(WINDOW, (e + 1) * tile)]
        for t in range(step // tile):
            wst[1 + e : 2 + e, t * tile : t * tile + part.shape[1]] = part
    load(SLOTS - 1).start()
    pl.semaphore_wait(barrier, len(peers))

    def compute(i, dst):
        load(i).wait()
        block = base(steps[i]) // width
        gate = keep_ref[pl.ds(block, 1), :].astype(jnp.float32)
        masked[...] = (panel[...] * gate).astype(jnp.bfloat16)
        first_row = lax.broadcasted_iota(jnp.int32, (STAT, SUB), 0) == 0

        def body(j, carry):
            at = pl.multiple_of(j * SUB, SUB)
            piece = mbuf[i % SLOTS, :, pl.ds(at, SUB)]
            dst[pl.ds(0, WINDOW), pl.ds(at, SUB)] = jnp.dot(
                masked[...], piece, preferred_element_type=jnp.float32
            )
            wide = piece.astype(jnp.float32)
            sq = jnp.sum(wide * wide, axis=0, keepdims=True)
            dst[pl.ds(WINDOW, STAT), pl.ds(at, SUB)] = jnp.where(
                first_row, sq, wst[:, pl.ds(at, SUB)]
            )
            return carry

        lax.fori_loop(0, step // SUB, body, 0)
        if i + SLOTS < len(steps):
            load(i + SLOTS).start()

    list_a, list_b, list_z = pieces()
    sends = {}
    buf_of = {}
    nsem = 0
    nbuf = 0
    for p in list_a + list_b + list_z:
        for phase in range(3):
            axis, kept, sent = phase_copies(p.order, phase, cfg)
            if not sent:
                buf_of[p, phase] = None
                sends[p, phase] = {}
                continue
            ref = bufs[nbuf]
            nbuf += 1
            buf_of[p, phase] = ref
            done = "z" in p.order[:phase]
            out = {}
            for d in range(1, cfg[axis] if axis != "z" else Z):
                for k, g in enumerate(sent[d - 1]):
                    if axis == "z":
                        to = lax.rem(z + d, Z)
                        cols = pl.ds(pl.multiple_of(to * tile, tile), tile)
                    elif done:
                        cols = pl.ds(pl.multiple_of(z * tile, tile), tile)
                    else:
                        cols = pl.ds(0, span)
                    copy = functools.partial(
                        pltpu.make_async_remote_copy,
                        src_ref=acc.at[quad(g), pl.ds(p.start, p.height), cols],
                        dst_ref=ref.at[d - 1, k],
                        send_sem=send_sem.at[nsem],
                        recv_sem=recv_sem.at[nsem],
                        device_id=peer(axis, d),
                        device_id_type=MESH,
                    )
                    nsem += 1
                    out.setdefault(g, []).append(copy)
            sends[p, phase] = out

    def start(p, phase, g=None):
        for key, copies in sends[p, phase].items():
            if g is None or key == g:
                for copy in copies:
                    copy().start()

    def finish(p, phase):
        axis, kept, sent = phase_copies(p.order, phase, cfg)
        for copies in sends[p, phase].values():
            for copy in copies:
                copy().wait_recv()
        if not sent:
            return
        ref = buf_of[p, phase]
        if "z" in p.order[: phase + 1]:
            cols = pl.ds(pl.multiple_of(z * tile, tile), tile)
        else:
            cols = pl.ds(0, span)
        for k, g in enumerate(kept):
            where = (quad(g), pl.ds(p.start, p.height), cols)
            total = acc[where]
            for d in range(len(sent)):
                total = total + ref[d, k]
            acc[where] = total

    def sibling(gi, h):
        n = gi * halves + h
        return pltpu.make_async_remote_copy(
            src_ref=sib_out.at[n],
            dst_ref=sib_in.at[n],
            send_sem=sib_send.at[n],
            recv_sem=sib_recv.at[n],
            device_id=device(y, x, 1 - c, z),
            device_id_type=MESH,
        )

    early = list_z + [p for pair in zip(list_a[:EARLY], list_b[:EARLY]) for p in pair]
    i = 0
    for gi, g in enumerate(groups):
        for h in range(halves):
            compute(i, sib_out.at[gi * halves + h])
            i += 1
            sibling(gi, h).start()
        q = quad(g)
        for h in range(halves):
            compute(i, acc.at[q, :, pl.ds(h * step, step)])
            i += 1
        for h in range(halves):
            sibling(gi, h).wait_recv()

            def add(j, carry, h=h, gi=gi, q=q):
                at = pl.multiple_of(j * 8, 8)
                acc[q, pl.ds(at, 8), pl.ds(h * step, step)] += sib_in[
                    gi * halves + h, pl.ds(at, 8), :
                ]
                return carry

            lax.fori_loop(0, HEIGHT // 8, add, 0)
        for p in early:
            start(p, 0, g)

    count = len(list_a)
    for t in range(count + 2):
        if EARLY <= t + 1 < count:
            start(list_a[t + 1], 0)
            start(list_b[t + 1], 0)
        if t < count:
            for p in (list_a[t], list_b[t]):
                finish(p, 0)
                start(p, 1)
        if t == 0 or t == 1:
            for p in list_z:
                finish(p, t)
                start(p, t + 1)
        if 1 <= t <= count:
            for p in (list_a[t - 1], list_b[t - 1]):
                finish(p, 1)
                start(p, 2)
        if t == 2:
            for p in list_z:
                finish(p, 2)
        if t >= 2:
            for p in (list_a[t - 2], list_b[t - 2]):
                finish(p, 2)

    mine = acc[y * X + x, :, pl.ds(pl.multiple_of(z * tile, tile), tile)]
    own = 1.0 / jnp.sqrt(mine[WINDOW : WINDOW + 1, :] + 1e-06)
    parts = [
        mine[WINDOW + 1 + e : WINDOW + 2 + e, : min(tile, WINDOW - e * tile)]
        for e in range(extra)
    ]
    win = parts[0] if extra == 1 else jnp.concatenate(parts, axis=1)
    win = 1.0 / jnp.sqrt(win + 1e-06)
    out_ref[...] = (mine[:WINDOW, :] * own).T * win

    for gi in range(len(groups)):
        for h in range(halves):
            sibling(gi, h).wait_send()
    for p in list_a + list_b + list_z:
        for phase in range(3):
            for copies in sends[p, phase].values():
                for copy in copies:
                    copy().wait_send()


def shards(matrix, keep_mask):
    depth, columns = matrix.shape
    blocks = keep_mask.shape[0]
    width = columns // blocks
    outer = lax.axis_size("rows")
    inner = lax.axis_size("grp")
    tile = columns // (outer * inner)
    cfg = {"x": 2, "y": outer // 4, "z": inner, "tile": tile, "width": width}
    span = inner * tile
    step = min(width, span)
    cfg["step"] = step
    quads = cfg["x"] * cfg["y"]
    links = quads * (span // step)
    bufs, nsem = [], 0
    for group in pieces():
        for p in group:
            for phase in range(3):
                axis, kept, sent = phase_copies(p.order, phase, cfg)
                if not sent:
                    continue
                cols = tile if "z" in p.order[: phase + 1] else span
                nsem += len(sent) * len(kept)
                bufs.append(
                    pltpu.VMEM((len(sent), len(kept), p.height, cols), jnp.float32)
                )
    return pl.pallas_call(
        functools.partial(kernel, cfg),
        out_shape=jax.ShapeDtypeStruct((tile, WINDOW), jnp.float32),
        in_specs=[
            pl.BlockSpec(memory_space=pl.ANY),
            pl.BlockSpec(memory_space=pltpu.VMEM),
        ],
        out_specs=pl.BlockSpec(memory_space=pltpu.VMEM),
        scratch_shapes=[
            pltpu.VMEM((quads, HEIGHT, span), jnp.float32),
            pltpu.VMEM((links, HEIGHT, step), jnp.float32),
            pltpu.VMEM((links, HEIGHT, step), jnp.float32),
            pltpu.VMEM((SLOTS, depth, step), jnp.bfloat16),
            pltpu.VMEM((WINDOW, depth), jnp.float32),
            pltpu.VMEM((WINDOW, depth), jnp.bfloat16),
            pltpu.VMEM((STAT, step), jnp.float32),
            pltpu.SemaphoreType.DMA((SLOTS,)),
            pltpu.SemaphoreType.DMA((links,)),
            pltpu.SemaphoreType.DMA((links,)),
            pltpu.SemaphoreType.DMA((nsem,)),
            pltpu.SemaphoreType.DMA((nsem,)),
        ]
        + bufs,
        compiler_params=pltpu.CompilerParams(
            collective_id=0, has_side_effects=True, vmem_limit_bytes=62 * 1024 * 1024
        ),
        cost_estimate=pl.CostEstimate(
            flops=2 * depth * columns * WINDOW,
            bytes_accessed=2 * depth * columns,
            transcendentals=0,
        ),
    )(matrix, keep_mask)


def solution(mesh):
    in_specs = (P(("rows", "grp"), None), P(None, ("rows", "grp")))
    out_specs = P(("rows", "grp"), None)
    return jax.shard_map(shards, mesh=mesh, in_specs=in_specs, out_specs=out_specs, check_vma=False)
```

time: 271 us -> 91.9 us (0.34)
  waiting for transfers between devices: 168 us -> 0 us
  Pallas kernels: 0 us -> 89.8 us
  other arithmetic: 52.2 us -> 0 us
  local copies, waits for them, and re-layouts: 21.2 us -> 1.87 us
  matrix products: 15 us -> 0 us
  between operations: 13.5 us -> 0.01 us
    reduce_scatter x2 -> x0, waiting for transfers between devices: 168 us -> none  [the longest x1 121 us: shards(): lax.psum_scatter(jnp.concatenate([product, stats], axis=1), 'rows', scatt...]
    pallas_call x0 -> x1, Pallas kernels: none -> 89.8 us  [shards(): pl.pallas_call(functools.partial(kernel, cfg), out_shape=jax.ShapeDtypeSt...]
    mul x2 -> x0, other arithmetic: 28.1 us -> none  [the longest x1 26.9 us: shards(): matrix.reshape(rows_here, blocks, width) * gate[:, :, None]]
    unnamed x5 -> x1, local copies, waits for them, and re-layouts: 17.5 us -> 1.87 us
    dot_general x1 -> x0, matrix products: 15 us -> none  [shards(): lax.dot_general(masked, panel, (((0,), (0,)), ((), ())), preferred_elemen...]
    concatenate x1 -> x0, other arithmetic: 11.7 us -> none  [shards(): jnp.concatenate([product, stats], axis=1)]
    reduce_sum x1 -> x0, other arithmetic: 10.2 us -> none  [shards(): square = jnp.sum(jnp.square(matrix.astype(jnp.float32)), axis=0)]
    mul x2 -> x0, local copies, waits for them, and re-layouts: 3.57 us -> none  [the longest x1 2.58 us: shards(): matrix.reshape(rows_here, blocks, width) * gate[:, :, None]]
  transfers between devices with their start and end apart: 2 -> 0, of which waited for: 2 -> 0; matrix products, arithmetic and copies ran while one was open for 0% -> 0% of each run, Pallas kernels for 0% -> 0%
where the time goes in v1:
time: 91.9 us; the launch traced here: 91.7 us
  Pallas kernels  89.8 us (98%)
  local copies, waits for them, and re-layouts  1.87 us (2%)
    pallas_call x1, Pallas kernels, shards(): pl.pallas_call(functools.partial(kernel, cfg), out_shape=jax.ShapeDtypeSt...  89.8 us
    unnamed x1, local copies, waits for them, and re-layouts  1.87 us

profile of v1, /device:TPU:0, one launch (start us, length us, event | category | flops | bytes accessed | tf_op | source)
XLA Modules:
  0.0 91.7 jit_solution(9569786263448031587)
XLA Ops:
  0.0 89.8 %shard_map.28 = f32[512,256]{1,0:T(8,128)} custom-call(bf16[768,16384]{1,0:T(8,128)(2,1)} %matrix_ref.1, s32[16,768]{1,0:T(8,128)} %keep_ref.1), custom_call_target="tpu_custom_call" | custom-call | flops 6442450944 | bytes 25165824 | tf_op jit(solution)/shard_map/pallas_call | solution.py:330
  89.8 1.9 %copy.4 = f32[512,256]{1,0:T(8,128)} copy(f32[512,256]{1,0:T(8,128)} %shard_map.28) | data formatting | bytes 1048576
